TPU v7x, 32 devices: a whole 2x2x4 slice. The times are simulated.
32 devices in a mesh: loc: 32 (over z, y, x, core).
Axes of the slice: x: 2, y: 2, z: 4, core: 2. Of those that a mesh axis runs over, the one named last changes fastest.
Arguments:
- hazard_bins: int32 [256, 8192], P(None, 'loc'), may hold values from 0 to 63
- curve_index: int32 [8192], P('loc'), may hold values from 0 to 255
- damage_table: float32 [256, 64], replicated, may hold values from 0.02 to 0.9
- insured_value: float32 [8192], P('loc'), may hold values from 0.5 to 5
- deductible: float32 [8192], P('loc'), may hold values from 0.05 to 0.5
- loss_limit: float32 [8192], P('loc'), may hold values from 0.5 to 3
- uncertainty: float32 [128, 8192], P(None, 'loc'), may hold values from 0.5 to 2
- year_ids: int32 [256], replicated, may hold values from 0 to 63
Outputs:
- event_loss: float32 [256, 128], P('loc')
- year_loss: float32 [64, 128], replicated
All inputs are finite; a program needn't handle non-finite values.
Results may differ from a plain program's by a relative error of at most 0.00005.
Values sent between devices are 32-bit elements; how exact they have to be, the bound alone decides.
A program may use at most 64 MiB of HBM per device.

v0:
```python
import math

import jax
import jax.numpy as jnp
from jax import lax
from jax.sharding import PartitionSpec as P

YEARS = 64


def shards(
    hazard_bins,
    curve_index,
    damage_table,
    insured_value,
    deductible,
    loss_limit,
    uncertainty,
    year_ids,
):
    curve_count = damage_table.shape[0]
    bin_count = damage_table.shape[1]
    selector = (curve_index[None, :] == jnp.arange(curve_count, dtype=jnp.int32)[:, None]).astype(
        jnp.float32
    )
    curve_rows = jnp.dot(
        damage_table.T,
        selector,
        precision=lax.Precision.HIGHEST,
        preferred_element_type=jnp.float32,
    )
    bin_ids = jnp.arange(bin_count, dtype=jnp.int32)[None, :, None]
    shard_width = insured_value.shape[0]
    locations = shard_width * lax.axis_size("loc")
    event_total = hazard_bins.shape[0]
    own_rows = event_total // lax.axis_size("loc")
    year_range = jnp.arange(YEARS, dtype=jnp.int32)
    target_rows = max(16, 32768 // shard_width)
    target_rows = 1 << target_rows.bit_length() - 1

    def block_terms(hazard_block):
        ratios = jnp.sum(
            jnp.where(hazard_block[:, None, :] == bin_ids, curve_rows[None, :, :], 0.0), axis=1
        )
        damage = jnp.minimum(ratios[:, None, :] * uncertainty[None, :, :], 1.0)
        losses = jnp.minimum(jnp.maximum(insured_value * damage - deductible, 0.0), loss_limit)
        return jnp.sum(losses, axis=2)

    block_rows = math.gcd(event_total, target_rows)
    grouped = hazard_bins.reshape(event_total // block_rows, block_rows, hazard_bins.shape[1])
    summed = lax.psum(
        lax.map(block_terms, grouped).reshape(event_total, uncertainty.shape[0]), "loc"
    )
    all_events = summed * (1.0 / locations)
    membership = (year_ids[:, None] == year_range[None, :]).astype(jnp.float32)
    year_loss = jnp.dot(
        membership.T,
        all_events,
        precision=lax.Precision.HIGHEST,
        preferred_element_type=jnp.float32,
    ) * (YEARS / event_total)
    event_loss = lax.dynamic_slice_in_dim(all_events, lax.axis_index("loc") * own_rows, own_rows, 0)
    return (event_loss, year_loss)


def solution(mesh):
    return jax.shard_map(
        shards,
        mesh=mesh,
        in_specs=(P(None, "loc"), P("loc"), P(), P("loc"), P("loc"), P("loc"), P(None, "loc"), P()),
        out_specs=(P("loc", None), P()),
        check_vma=False,
    )
```

profile of v0, /device:TPU:0, one launch (start us, length us, event | category | flops | bytes accessed | tf_op | source)
XLA Modules:
  0.0 161.2 jit_solution(17336315742773112577)
XLA Ops:
  7.2 0.0 copy-start
  7.2 0.0 all-reduce.2.cloned.1.call-start
  7.2 0.8 copy-done
  8.0 0.9 convolution_bitcast_fusion
  8.9 14.9 %while.11 = (s32[]{:T(128)}, f32[2,128,128]{2,1,0:T(8,128)S(1)}, f32[256]{0:T(256)}, s32[2,128,256]{2,1,0:T(8,128)}, f32[64,256]{1,0:T(8,128)S(1)}, /*index=5*/f...) while((s32[]{:T(128)}, f32[2,128,128]{2,1,0:T(8,128)S(1)}, f32[256]{0:T(256)}, ...), condition=%wide.region_3.4_spmd.clone, body=%wide.region_0.3_spmd.clone.sunk | while | flops 35602432 | bytes 1588437 | solution.py:52
  8.9 0.0 copy-start.1
  8.9 0.0 copy-start.4
  9.0 0.0 copy-start.5
  9.0 0.0 copy-start.6
  9.0 1.0 dynamic-slice_bitcast_fusion.2
  10.0 2.4 %select_reduce_fusion.2 = f32[128,256]{1,0:T(8,128)S(1)} fusion(f32[64,256]{1,0:T(8,128)S(1)} %get-tuple-element.155, s32[128,256]{1,0:T(8,128)S(1)} %dynamic-slice_bitcast_fusion.2), kind=kLoop, calls=%fused_computation.3.clone.1 | loop fusion | flops 6258688 | bytes 327680 | tf_op jit(solution)/shard_map/while/body/eval_jaxpr/reduce_sum | solution.py:42
  12.4 0.0 copy-done.1
  12.4 0.0 copy-done.4
  12.4 0.0 copy-done.5
  12.4 0.0 copy-done.6
  12.4 3.9 %minimum_reduce_fusion.2 = f32[128,128]{1,0:T(8,128)S(1)} fusion(f32[256]{0:T(256)S(1)} %copy-done.6, f32[256]{0:T(256)S(1)} %copy-done.5, f32[128,256]{1,0:T(8,128)S(1)} %copy-done.1, f32[128,256]{1,0:T(8,128)S(1)} %select_reduce_fusion.2, f32[256]{0:T(256)S(1)} %copy-done.4), kind=kLoop, calls=%fused_computation.1.clone.1 | loop fusion | flops 29343744 | bytes 330752 | tf_op jit(solution)/shard_map/while/body/eval_jaxpr/reduce_sum | solution.py:47
  16.4 0.0 copy-start.1
  16.4 0.0 copy-start.4
  16.4 0.0 copy-start.5
  16.4 0.0 copy-start.6
  16.4 1.0 dynamic-slice_bitcast_fusion.2
  17.4 2.4 %select_reduce_fusion.2 = f32[128,256]{1,0:T(8,128)S(1)} fusion(f32[64,256]{1,0:T(8,128)S(1)} %get-tuple-element.155, s32[128,256]{1,0:T(8,128)S(1)} %dynamic-slice_bitcast_fusion.2), kind=kLoop, calls=%fused_computation.3.clone.1 | loop fusion | flops 6258688 | bytes 327680 | tf_op jit(solution)/shard_map/while/body/eval_jaxpr/reduce_sum | solution.py:42
  19.8 0.0 copy-done.1
  19.8 0.0 copy-done.4
  19.8 0.0 copy-done.5
  19.8 0.0 copy-done.6
  19.8 3.9 %minimum_reduce_fusion.2 = f32[128,128]{1,0:T(8,128)S(1)} fusion(f32[256]{0:T(256)S(1)} %copy-done.6, f32[256]{0:T(256)S(1)} %copy-done.5, f32[128,256]{1,0:T(8,128)S(1)} %copy-done.1, f32[128,256]{1,0:T(8,128)S(1)} %select_reduce_fusion.2, f32[256]{0:T(256)S(1)} %copy-done.4), kind=kLoop, calls=%fused_computation.1.clone.1 | loop fusion | flops 29343744 | bytes 330752 | tf_op jit(solution)/shard_map/while/body/eval_jaxpr/reduce_sum | solution.py:47
  23.8 0.0 copy-start.3
  23.8 0.0 copy-start.7
  23.8 0.6 copy-done.3
  24.4 0.0 all-reduce.2.cloned.1.call-update
  24.4 127.3 %all-reduce.2.cloned.1.call-done = f32[256,128]{1,0:T(8,128)} async-done(((f32[256,128]{1,0:T(8,128)}), f32[256,128]{1,0:T(8,128)}) %all-reduce.2.cloned.1.call-update) | async-done | bytes 131088 | tf_op jit(solution)/shard_map/psum | solution.py:51
  151.8 0.0 copy-start.2
  151.8 1.0 broadcast_multiply_fusion
  152.8 0.6 constant_dynamic-slice_fusion
  153.4 0.0 copy-done.7
  153.4 0.0 copy-done.2
  153.4 1.0 convolution_multiply_fusion
  (3 shorter events, 0.0 us)
Async XLA Ops:
  7.2 0.8 copy-start
  7.2 144.6 %all-reduce.2.cloned.1.call-start = ((), (), s32[]{:S(2)}) async-start(), calls=%async_computation | async-start | bytes 262144 | tf_op jit(solution)/shard_map/psum | solution.py:51
  8.9 3.4 %copy-start.1 = (f32[128,256]{1,0:T(8,128)S(1)}, f32[128,256]{1,0:T(8,128)}, u32[]{:S(2)}) copy-start(f32[128,256]{1,0:T(8,128)} %get-tuple-element.156) | copy-start | bytes 393220 | tf_op jit(solution)/shard_map/while
  8.9 3.4 %copy-start.4 = (f32[256]{0:T(256)S(1)}, f32[256]{0:T(256)}, u32[]{:S(2)}) copy-start(f32[256]{0:T(256)} %get-tuple-element.153) | copy-start | bytes 3076 | tf_op jit(solution)/shard_map/while
  9.0 3.4 %copy-start.5 = (f32[256]{0:T(256)S(1)}, f32[256]{0:T(256)}, u32[]{:S(2)}) copy-start(f32[256]{0:T(256)} %get-tuple-element.157) | copy-start | bytes 3076 | tf_op jit(solution)/shard_map/while
  9.0 3.4 %copy-start.6 = (f32[256]{0:T(256)S(1)}, f32[256]{0:T(256)}, u32[]{:S(2)}) copy-start(f32[256]{0:T(256)} %get-tuple-element.158) | copy-start | bytes 3076 | tf_op jit(solution)/shard_map/while
  16.4 3.4 %copy-start.1 = (f32[128,256]{1,0:T(8,128)S(1)}, f32[128,256]{1,0:T(8,128)}, u32[]{:S(2)}) copy-start(f32[128,256]{1,0:T(8,128)} %get-tuple-element.156) | copy-start | bytes 393220 | tf_op jit(solution)/shard_map/while
  16.4 3.4 %copy-start.4 = (f32[256]{0:T(256)S(1)}, f32[256]{0:T(256)}, u32[]{:S(2)}) copy-start(f32[256]{0:T(256)} %get-tuple-element.153) | copy-start | bytes 3076 | tf_op jit(solution)/shard_map/while
  16.4 3.4 %copy-start.5 = (f32[256]{0:T(256)S(1)}, f32[256]{0:T(256)}, u32[]{:S(2)}) copy-start(f32[256]{0:T(256)} %get-tuple-element.157) | copy-start | bytes 3076 | tf_op jit(solution)/shard_map/while
  16.4 3.4 %copy-start.6 = (f32[256]{0:T(256)S(1)}, f32[256]{0:T(256)}, u32[]{:S(2)}) copy-start(f32[256]{0:T(256)} %get-tuple-element.158) | copy-start | bytes 3076 | tf_op jit(solution)/shard_map/while
  23.8 0.6 copy-start.3
  23.8 129.6 %copy-start.7 = (s32[256]{0:T(256)S(1)}, s32[256]{0:T(256)}, u32[]{:S(2)}) copy-start(s32[256]{0:T(256)} %param.17) | copy-start | bytes 3076
  151.8 1.6 copy-start.2
Sparse Core Ops, SparseCore 0:
  24.6 127.1 all-reduce.1
where the time goes:
time: 161 us
  waiting for transfers between devices  127 us (79%)
  between operations  14.1 us (9%)
  other arithmetic  13.6 us (8%)
  local copies, waits for them, and re-layouts  4.04 us (3%)
  matrix products  1.85 us (1%)
    psum x1, waiting for transfers between devices, shards(): lax.psum(lax.map(block_terms, grouped).reshape(event_total, uncertainty.s...  127 us
    reduce_sum x2, other arithmetic, block_terms(): return jnp.sum(losses, axis=2)  7.85 us
    reduce_sum x2, other arithmetic, block_terms(): jnp.sum(jnp.where(hazard_block[:, None, :] == bin_ids, curve_rows[None, :...  4.8 us
  transfers between devices with their start and end apart: 1, of which 1 were waited for; matrix products, arithmetic and copies ran while one was open for 0% of the time, Pallas kernels for 0%

commit v1 on v0

v1 whole, which is shorter than its diff:
```python
import functools
import math

import jax
import jax.numpy as jnp
from jax import lax
from jax.experimental import pallas as pl
from jax.experimental.pallas import tpu as pltpu
from jax.sharding import PartitionSpec as P

YEARS = 64
BIN_CHUNK = 8
MESH = pl.DeviceIdType.MESH
F32 = jnp.float32
BF16 = jnp.bfloat16
NT = (((1,), (1,)), ((), ()))


def split3(x):
    a = x.astype(BF16)
    rest = x - a.astype(F32)
    b = rest.astype(BF16)
    c = (rest - b.astype(F32)).astype(BF16)
    return a, b, c


def kernel(
    n,
    group,
    h_ref,
    ci_ref,
    tab_ref,
    iv_ref,
    d_ref,
    lim_ref,
    u_ref,
    yid_ref,
    ev_ref,
    yr_ref,
    hb,
    rt,
    v,
    acc,
    out1,
    in1,
    out2,
    in2,
    out3,
    in3,
    send1,
    recv1,
    send2,
    recv2,
    send3,
    recv3,
):
    planes = n // group
    events, width = h_ref.shape
    samples = u_ref.shape[0]
    curves, bins = tab_ref.shape
    own = events // n
    years = yr_ref.shape[0]
    yown = years // group
    me = lax.axis_index("loc")
    q = me // group
    p = me % group

    def in_group(k):
        return q * group + (p + k) % group

    def in_line(k):
        return ((q + k) % planes) * group + p

    barrier = pltpu.get_barrier_semaphore()
    for k in range(1, group):
        pl.semaphore_signal(barrier, inc=1, device_id=(in_group(k),), device_id_type=MESH)
    for k in range(1, planes):
        pl.semaphore_signal(barrier, inc=1, device_id=(in_line(k),), device_id_type=MESH)

    selector = (
        (lax.broadcasted_iota(jnp.int32, (curves, width), 0) == ci_ref[...])
        .astype(F32)
        .astype(BF16)
    )
    parts = jnp.concatenate(split3(tab_ref[...].T), axis=0)
    picked = jnp.dot(parts, selector, preferred_element_type=F32)
    rt[...] = picked[:bins] + picked[bins : 2 * bins] + picked[2 * bins :]
    v[...] = u_ref[...] * iv_ref[...]
    hb[...] = h_ref[...].astype(F32).astype(BF16)
    acc[...] = jnp.zeros_like(acc)
    cap_row = jnp.maximum(jnp.minimum(lim_ref[...], iv_ref[...] - d_ref[...]), 0.0)
    d_row = d_ref[...]

    @pl.loop(0, bins // BIN_CHUNK)
    def _(c):
        base = pl.multiple_of(c * BIN_CHUNK, BIN_CHUNK)
        rows = rt[pl.ds(base, BIN_CHUNK), :]
        shifted = hb[...] - jnp.full((1, width), base.astype(F32), F32).astype(BF16)
        hots, terms = [], []
        for j in range(BIN_CHUNK):
            x = rows[j : j + 1, :] * v[...] - d_row
            x = jnp.minimum(jnp.maximum(x, 0.0), cap_row)
            hi = x.astype(BF16)
            lo = (x - hi.astype(F32)).astype(BF16)
            terms.append(jnp.concatenate([hi, lo], axis=0))
            hots.append(jnp.where(shifted == BF16(j), BF16(1), BF16(0)))
        acc[...] += lax.dot_general(
            jnp.concatenate(hots, axis=1),
            jnp.concatenate(terms, axis=1),
            NT,
            preferred_element_type=F32,
        )

    scale = 1.0 / (width * n)
    sums = (acc[:, :samples] + acc[:, samples:]) * scale
    member = (
        (lax.broadcasted_iota(jnp.int32, (years, events), 0) == yid_ref[...])
        .astype(F32)
        .astype(BF16)
    )
    ysums = jnp.dot(
        member, jnp.concatenate(split3(sums), axis=1), preferred_element_type=F32
    )
    ysums = ysums[:, :samples] + ysums[:, samples : 2 * samples] + ysums[:, 2 * samples :]
    ysums = ysums * (years / events)
    for t in range(planes):
        for g in range(group):
            at = (t * group + g) * own
            out1[g, t * own : (t + 1) * own, :] = sums[at : at + own, :]
    for g in range(group):
        out1[g, planes * own :, :] = ysums[g * yown : (g + 1) * yown, :]

    pl.semaphore_wait(barrier, group - 1 + planes - 1)

    copies = []
    for k in range(1, group):
        copies.append(
            pltpu.make_async_remote_copy(
                src_ref=out1.at[(p + k) % group],
                dst_ref=in1.at[k - 1],
                send_sem=send1.at[k - 1],
                recv_sem=recv1.at[k - 1],
                device_id=(in_group(k),),
                device_id_type=MESH,
            )
        )
        copies[-1].start()
    total = out1[p]
    for k in range(1, group):
        copies[k - 1].wait_recv()
        total = total + in1[k - 1]

    for t in range(planes):
        out2[t, :own, :] = total[t * own : (t + 1) * own, :]
        out2[t, own:, :] = total[planes * own :, :]
    second = []
    for k in range(1, planes):
        second.append(
            pltpu.make_async_remote_copy(
                src_ref=out2.at[(q + k) % planes],
                dst_ref=in2.at[q],
                send_sem=send2.at[k - 1],
                recv_sem=recv2.at[k - 1],
                device_id=(in_line(k),),
                device_id_type=MESH,
            )
        )
        second[-1].start()
    in2[q] = out2[q]
    for copy in second:
        copy.wait_recv()
    done = in2[0]
    for t in range(1, planes):
        done = done + in2[t]
    out3[...] = done[own:, :]
    third = []
    for k in range(1, group):
        third.append(
            pltpu.make_async_remote_copy(
                src_ref=out3,
                dst_ref=in3.at[p],
                send_sem=send3.at[k - 1],
                recv_sem=recv3.at[k - 1],
                device_id=(in_group(k),),
                device_id_type=MESH,
            )
        )
        third[-1].start()
    ev_ref[...] = done[:own, :]
    in3[p] = done[own:, :]
    for copy in third:
        copy.wait_recv()
    for g in range(group):
        yr_ref[g * yown : (g + 1) * yown, :] = in3[g]
    for copy in copies + second + third:
        copy.wait_send()


def shards(n, hazard, curve, table, value, deductible, limit, uncertainty, year_ids):
    events, width = hazard.shape
    samples = uncertainty.shape[0]
    bins = table.shape[1]
    group = math.gcd(n, 8)
    planes = n // group
    own = events // n
    yown = YEARS // group
    row = lambda a: a.reshape(1, a.shape[0])
    dma = pltpu.SemaphoreType.DMA
    return pl.pallas_call(
        functools.partial(kernel, n, group),
        out_shape=(
            jax.ShapeDtypeStruct((own, samples), F32),
            jax.ShapeDtypeStruct((YEARS, samples), F32),
        ),
        in_specs=[pl.BlockSpec(memory_space=pltpu.VMEM)] * 8,
        out_specs=(pl.BlockSpec(memory_space=pltpu.VMEM),) * 2,
        scratch_shapes=[
            pltpu.VMEM((events, width), BF16),
            pltpu.VMEM((bins, width), F32),
            pltpu.VMEM((samples, width), F32),
            pltpu.VMEM((events, 2 * samples), F32),
            pltpu.VMEM((group, planes * own + yown, samples), F32),
            pltpu.VMEM((group - 1, planes * own + yown, samples), F32),
            pltpu.VMEM((planes, own + yown, samples), F32),
            pltpu.VMEM((planes, own + yown, samples), F32),
            pltpu.VMEM((yown, samples), F32),
            pltpu.VMEM((group, yown, samples), F32),
            dma((group - 1,)),
            dma((group - 1,)),
            dma((planes - 1,)),
            dma((planes - 1,)),
            dma((group - 1,)),
            dma((group - 1,)),
        ],
        compiler_params=pltpu.CompilerParams(collective_id=0, has_side_effects=True),
    )(
        hazard,
        row(curve),
        table,
        row(value),
        row(deductible),
        row(limit),
        uncertainty,
        row(year_ids),
    )


def solution(mesh):
    n = mesh.shape["loc"]
    return jax.shard_map(
        functools.partial(shards, n),
        mesh=mesh,
        in_specs=(P(None, "loc"), P("loc"), P(), P("loc"), P("loc"), P("loc"), P(None, "loc"), P()),
        out_specs=(P("loc", None), P()),
        check_vma=False,
    )
```

time: 161 us -> 25.5 us (0.16)
  waiting for transfers between devices: 127 us -> 0 us
  Pallas kernels: 0 us -> 20.4 us
  other arithmetic: 13.6 us -> 0 us
  between operations: 14.1 us -> 0.64 us
  matrix products: 1.85 us -> 0 us
    psum x1 -> x0, waiting for transfers between devices: 127 us -> none  [shards(): lax.psum(lax.map(block_terms, grouped).reshape(event_total, uncertainty.s...]
    pallas_call x0 -> x1, Pallas kernels: none -> 20.4 us  [shards(): pl.pallas_call(functools.partial(kernel, n, group), out_shape=(jax.ShapeD...]
    reduce_sum x4 -> x0, other arithmetic: 12.7 us -> none  [the longest x2 7.85 us: block_terms(): return jnp.sum(losses, axis=2)]
    unnamed x8 -> x3, local copies, waits for them, and re-layouts: 1.41 us -> 4.24 us
    eq x2 -> x0, local copies, waits for them, and re-layouts: 1.95 us -> none  [block_terms(): hazard_block[:, None, :] == bin_ids]
    dot_general x2 -> x0, matrix products: 1.85 us -> none  [the longest x1 0.96 us: shards(): jnp.dot(membership.T, all_events, precision=lax.Precision.HIGHEST, prefer...]
  transfers between devices with their start and end apart: 1 -> 0, of which waited for: 1 -> 0; matrix products, arithmetic and copies ran while one was open for 0% -> 0% of each run, Pallas kernels for 0% -> 0%
where the time goes in v1:
time: 25.5 us; the launch traced here: 25.2 us
  Pallas kernels  20.4 us (80%)
  local copies, waits for them, and re-layouts  4.24 us (17%)
  between operations  0.64 us (3%)
    pallas_call x1, Pallas kernels, shards(): pl.pallas_call(functools.partial(kernel, n, group), out_shape=(jax.ShapeD...  20.4 us
    unnamed x3, local copies, waits for them, and re-layouts  4.24 us

profile of v1, /device:TPU:0, one launch (start us, length us, event | category | flops | bytes accessed | tf_op | source)
XLA Modules:
  0.0 25.2 jit_solution(2517953168393185948)
XLA Ops:
  0.6 1.6 %copy.10.tab_ref = f32[256,64]{1,0:T(8,128)} copy(f32[256,64]{0,1:T(8,128)} %param.10) | data formatting | bytes 131072 | tf_op args[2]
  2.2 20.4 %shard_map.95 = (f32[8,128]{1,0:T(8,128)}, f32[64,128]{1,0:T(8,128)}) custom-call(s32[256,256]{1,0:T(8,128)} %h_ref.1, s32[1,256]{1,0:T(1,128)} %bitcast.5, f32[256,64]{1,0:T(8,128)} %copy.10.tab_ref, f32[1,256]{1,0:T(1,128)} %bitcast.6, f32[1,256]{1,0:T(1,128)} %bitcast.7, f32[1,256]{1,0:T(1,128)} %bitcast.8, f32[128,256]{1,0:T(8,128)} %u_ref.1, ...), custom_call_target="tpu_custom_call" | custom-call | tf_op jit(solution)/shard_map/pallas_call | solution.py:209
  22.6 1.3 %copy.13 = f32[8,128]{1,0:T(8,128)} copy(f32[8,128]{1,0:T(8,128)} %get-tuple-element.4) | data formatting | bytes 8192
  23.9 1.4 %copy.14 = f32[64,128]{1,0:T(8,128)} copy(f32[64,128]{1,0:T(8,128)} %get-tuple-element.5) | data formatting | bytes 65536

commit v2 on v1

--- a/solution.py
+++ b/solution.py
@@ -57,7 +57,7 @@
     planes = n // group
     events, width = h_ref.shape
     samples = u_ref.shape[0]
-    curves, bins = tab_ref.shape
+    bins, curves = tab_ref.shape
     own = events // n
     years = yr_ref.shape[0]
     yown = years // group
@@ -82,7 +82,7 @@
         .astype(F32)
         .astype(BF16)
     )
-    parts = jnp.concatenate(split3(tab_ref[...].T), axis=0)
+    parts = jnp.concatenate(split3(tab_ref[...]), axis=0)
     picked = jnp.dot(parts, selector, preferred_element_type=F32)
     rt[...] = picked[:bins] + picked[bins : 2 * bins] + picked[2 * bins :]
     v[...] = u_ref[...] * iv_ref[...]
@@ -208,10 +208,7 @@
     dma = pltpu.SemaphoreType.DMA
     return pl.pallas_call(
         functools.partial(kernel, n, group),
-        out_shape=(
-            jax.ShapeDtypeStruct((own, samples), F32),
-            jax.ShapeDtypeStruct((YEARS, samples), F32),
-        ),
+        out_shape=(pltpu.VMEM((own, samples), F32), pltpu.VMEM((YEARS, samples), F32)),
         in_specs=[pl.BlockSpec(memory_space=pltpu.VMEM)] * 8,
         out_specs=(pl.BlockSpec(memory_space=pltpu.VMEM),) * 2,
         scratch_shapes=[
@@ -236,7 +233,7 @@
     )(
         hazard,
         row(curve),
-        table,
+        table.T,
         row(value),
         row(deductible),
         row(limit),

time: 25.5 us -> 21.7 us (0.85)
  local copies, waits for them, and re-layouts: 4.24 us -> 1.21 us
  Pallas kernels: 20.4 us -> 19.7 us
    unnamed x3 -> x2, local copies, waits for them, and re-layouts: 4.24 us -> 1.21 us
    pallas_call x1, Pallas kernels: 20.4 us -> 19.7 us  [shards(): pl.pallas_call(functools.partial(kernel, n, group), out_shape=(pltpu.VMEM...]
where the time goes in v2:
time: 21.7 us; the launch traced here: 21.5 us
  Pallas kernels  19.7 us (91%)
  local copies, waits for them, and re-layouts  1.21 us (6%)
  between operations  0.64 us (3%)
    pallas_call x1, Pallas kernels, shards(): pl.pallas_call(functools.partial(kernel, n, group), out_shape=(pltpu.VMEM...  19.7 us
    unnamed x2, local copies, waits for them, and re-layouts  1.21 us

profile of v2, /device:TPU:0, one launch (start us, length us, event | category | flops | bytes accessed | tf_op | source)
XLA Modules:
  0.0 21.5 jit_solution(10502096597485505902)
XLA Ops:
  0.6 19.7 %shard_map.95 = (f32[8,128]{1,0:T(8,128)S(1)}, f32[64,128]{1,0:T(8,128)S(1)}) custom-call(s32[256,256]{1,0:T(8,128)} %h_ref.1, s32[1,256]{1,0:T(1,128)} %bitcast.7, f32[64,256]{1,0:T(8,128)} %bitcast.6, f32[1,256]{1,0:T(1,128)} %bitcast.8, f32[1,256]{1,0:T(1,128)} %bitcast.9, f32[1,256]{1,0:T(1,128)} %bitcast.10, f32[128,256]{1,0:T(8,128)} %u_ref.1, ...), custom_call_target="tpu_custom_call" | custom-call | tf_op jit(solution)/shard_map/pallas_call | solution.py:209
  20.3 0.6 %copy.12 = f32[8,128]{1,0:T(8,128)} copy(f32[8,128]{1,0:T(8,128)S(1)} %get-tuple-element.2) | data formatting | bytes 8192
  20.9 0.6 %copy.13 = f32[64,128]{1,0:T(8,128)} copy(f32[64,128]{1,0:T(8,128)S(1)} %get-tuple-element.3) | data formatting | bytes 65536

commit v3 on v2

--- a/solution.py
+++ b/solution.py
@@ -132,47 +132,70 @@
 
     pl.semaphore_wait(barrier, group - 1 + planes - 1)
 
-    copies = []
-    for k in range(1, group):
-        copies.append(
-            pltpu.make_async_remote_copy(
-                src_ref=out1.at[(p + k) % group],
-                dst_ref=in1.at[k - 1],
-                send_sem=send1.at[k - 1],
-                recv_sem=recv1.at[k - 1],
-                device_id=(in_group(k),),
-                device_id_type=MESH,
+    cut = planes * own
+    event_rows, year_rows = pl.ds(0, cut), pl.ds(cut, yown)
+    event_row, year_row = pl.ds(0, own), pl.ds(own, yown)
+
+    def to_group(rows, first):
+        sent = []
+        for k in range(1, group):
+            sent.append(
+                pltpu.make_async_remote_copy(
+                    src_ref=out1.at[(p + k) % group, rows],
+                    dst_ref=in1.at[k - 1, rows],
+                    send_sem=send1.at[first + k - 1],
+                    recv_sem=recv1.at[first + k - 1],
+                    device_id=(in_group(k),),
+                    device_id_type=MESH,
+                )
             )
-        )
-        copies[-1].start()
-    total = out1[p]
-    for k in range(1, group):
-        copies[k - 1].wait_recv()
-        total = total + in1[k - 1]
-
+            sent[-1].start()
+        return sent
+
+    def to_line(rows, first):
+        sent = []
+        for k in range(1, planes):
+            sent.append(
+                pltpu.make_async_remote_copy(
+                    src_ref=out2.at[(q + k) % planes, rows],
+                    dst_ref=in2.at[q, rows],
+                    send_sem=send2.at[first + k - 1],
+                    recv_sem=recv2.at[first + k - 1],
+                    device_id=(in_line(k),),
+                    device_id_type=MESH,
+                )
+            )
+            sent[-1].start()
+        return sent
+
+    def group_sum(rows, sent):
+        total = out1[p, rows]
+        for k in range(1, group):
+            sent[k - 1].wait_recv()
+            total = total + in1[k - 1, rows]
+        return total
+
+    def line_sum(rows, sent):
+        in2[q, rows] = out2[q, rows]
+        for copy in sent:
+            copy.wait_recv()
+        total = in2[0, rows]
+        for t in range(1, planes):
+            total = total + in2[t, rows]
+        return total
+
+    years1 = to_group(year_rows, 0)
+    events1 = to_group(event_rows, group - 1)
+    total = group_sum(year_rows, years1)
+    for t in range(planes):
+        out2[t, own:, :] = total
+    years2 = to_line(year_row, 0)
+    total = group_sum(event_rows, events1)
     for t in range(planes):
         out2[t, :own, :] = total[t * own : (t + 1) * own, :]
-        out2[t, own:, :] = total[planes * own :, :]
-    second = []
-    for k in range(1, planes):
-        second.append(
-            pltpu.make_async_remote_copy(
-                src_ref=out2.at[(q + k) % planes],
-                dst_ref=in2.at[q],
-                send_sem=send2.at[k - 1],
-                recv_sem=recv2.at[k - 1],
-                device_id=(in_line(k),),
-                device_id_type=MESH,
-            )
-        )
-        second[-1].start()
-    in2[q] = out2[q]
-    for copy in second:
-        copy.wait_recv()
-    done = in2[0]
-    for t in range(1, planes):
-        done = done + in2[t]
-    out3[...] = done[own:, :]
+    events2 = to_line(event_row, planes - 1)
+    year_done = line_sum(year_row, years2)
+    out3[...] = year_done
     third = []
     for k in range(1, group):
         third.append(
@@ -186,13 +209,13 @@
             )
         )
         third[-1].start()
-    ev_ref[...] = done[:own, :]
-    in3[p] = done[own:, :]
+    in3[p] = year_done
+    ev_ref[...] = line_sum(event_row, events2)
     for copy in third:
         copy.wait_recv()
     for g in range(group):
         yr_ref[g * yown : (g + 1) * yown, :] = in3[g]
-    for copy in copies + second + third:
+    for copy in years1 + events1 + years2 + events2 + third:
         copy.wait_send()
 
 
@@ -222,10 +245,10 @@
             pltpu.VMEM((planes, own + yown, samples), F32),
             pltpu.VMEM((yown, samples), F32),
             pltpu.VMEM((group, yown, samples), F32),
-            dma((group - 1,)),
-            dma((group - 1,)),
-            dma((planes - 1,)),
-            dma((planes - 1,)),
+            dma((2 * (group - 1),)),
+            dma((2 * (group - 1),)),
+            dma((2 * (planes - 1),)),
+            dma((2 * (planes - 1),)),
             dma((group - 1,)),
             dma((group - 1,)),
         ],

time: 21.7 us -> 21.4 us (0.986)
  Pallas kernels: 19.7 us -> 19.4 us
    pallas_call x1, Pallas kernels: 19.7 us -> 19.4 us  [shards(): pl.pallas_call(functools.partial(kernel, n, group), out_shape=(pltpu.VMEM...]
where the time goes in v3:
time: 21.4 us; the launch traced here: 21.2 us
  Pallas kernels  19.4 us (91%)
  local copies, waits for them, and re-layouts  1.21 us (6%)
  between operations  0.64 us (3%)
    pallas_call x1, Pallas kernels, shards(): pl.pallas_call(functools.partial(kernel, n, group), out_shape=(pltpu.VMEM...  19.4 us
    unnamed x2, local copies, waits for them, and re-layouts  1.21 us

profile of v3, /device:TPU:0, one launch (start us, length us, event | category | flops | bytes accessed | tf_op | source)
XLA Modules:
  0.0 21.2 jit_solution(12123889276898898380)
XLA Ops:
  0.6 19.4 %shard_map.95 = (f32[8,128]{1,0:T(8,128)S(1)}, f32[64,128]{1,0:T(8,128)S(1)}) custom-call(s32[256,256]{1,0:T(8,128)} %h_ref.1, s32[1,256]{1,0:T(1,128)} %bitcast.7, f32[64,256]{1,0:T(8,128)} %bitcast.6, f32[1,256]{1,0:T(1,128)} %bitcast.8, f32[1,256]{1,0:T(1,128)} %bitcast.9, f32[1,256]{1,0:T(1,128)} %bitcast.10, f32[128,256]{1,0:T(8,128)} %u_ref.1, ...), custom_call_target="tpu_custom_call" | custom-call | tf_op jit(solution)/shard_map/pallas_call | solution.py:232
  20.0 0.6 %copy.12 = f32[8,128]{1,0:T(8,128)} copy(f32[8,128]{1,0:T(8,128)S(1)} %get-tuple-element.2) | data formatting | bytes 8192
  20.6 0.6 %copy.13 = f32[64,128]{1,0:T(8,128)} copy(f32[64,128]{1,0:T(8,128)S(1)} %get-tuple-element.3) | data formatting | bytes 65536

commit v4 on v3

--- a/solution.py
+++ b/solution.py
@@ -22,6 +22,10 @@
     b = rest.astype(BF16)
     c = (rest - b.astype(F32)).astype(BF16)
     return a, b, c
+
+
+def far_first(count):
+    return sorted(range(count), key=lambda k: abs(2 * k + 1 - count))
 
 
 def kernel(
@@ -149,7 +153,8 @@
                     device_id_type=MESH,
                 )
             )
-            sent[-1].start()
+        for k in far_first(len(sent)):
+            sent[k].start()
         return sent
 
     def to_line(rows, first):
@@ -165,7 +170,8 @@
                     device_id_type=MESH,
                 )
             )
-            sent[-1].start()
+        for k in far_first(len(sent)):
+            sent[k].start()
         return sent
 
     def group_sum(rows, sent):
@@ -208,7 +214,8 @@
                 device_id_type=MESH,
             )
         )
-        third[-1].start()
+    for k in far_first(len(third)):
+        third[k].start()
     in3[p] = year_done
     ev_ref[...] = line_sum(event_row, events2)
     for copy in third:

time: 21.4 us -> 21.4 us (level)
  no operation moved by 1% of the time
where the time goes in v4:
time: 21.4 us; the launch traced here: 21.3 us
  Pallas kernels  19.4 us (91%)
  local copies, waits for them, and re-layouts  1.21 us (6%)
  between operations  0.64 us (3%)
    pallas_call x1, Pallas kernels, shards(): pl.pallas_call(functools.partial(kernel, n, group), out_shape=(pltpu.VMEM...  19.4 us
    unnamed x2, local copies, waits for them, and re-layouts  1.21 us

profile of v4, /device:TPU:0, one launch (start us, length us, event | category | flops | bytes accessed | tf_op | source)
XLA Modules:
  0.0 21.3 jit_solution(2191733962510641854)
XLA Ops:
  0.6 19.4 %shard_map.95 = (f32[8,128]{1,0:T(8,128)S(1)}, f32[64,128]{1,0:T(8,128)S(1)}) custom-call(s32[256,256]{1,0:T(8,128)} %h_ref.1, s32[1,256]{1,0:T(1,128)} %bitcast.7, f32[64,256]{1,0:T(8,128)} %bitcast.6, f32[1,256]{1,0:T(1,128)} %bitcast.8, f32[1,256]{1,0:T(1,128)} %bitcast.9, f32[1,256]{1,0:T(1,128)} %bitcast.10, f32[128,256]{1,0:T(8,128)} %u_ref.1, ...), custom_call_target="tpu_custom_call" | custom-call | tf_op jit(solution)/shard_map/pallas_call | solution.py:239
  20.1 0.6 %copy.12 = f32[8,128]{1,0:T(8,128)} copy(f32[8,128]{1,0:T(8,128)S(1)} %get-tuple-element.2) | data formatting | bytes 8192
  20.7 0.6 %copy.13 = f32[64,128]{1,0:T(8,128)} copy(f32[64,128]{1,0:T(8,128)S(1)} %get-tuple-element.3) | data formatting | bytes 65536
